TPU v7x, 32 devices: a whole 2x2x4 slice. The times are simulated.
32 devices in a mesh: gx: 4 (over x, core), gy: 8 (over z, y).
Axes of the slice: x: 2, y: 2, z: 4, core: 2. Of those that a mesh axis runs over, the one named last changes fastest.
Arguments:
- populations: float32 [19, 32, 64, 128], P(None, 'gx', 'gy'), may hold values from 0 to 1, as said below
- cell_kind: int32 [32, 64, 128], P('gx', 'gy'), may hold values from 0 to 3, as said below
- outlet_region: int32 [32, 64], P('gx', 'gy'), may hold values from 0 to 63, as said below
Outputs:
- final_populations: float32 [19, 32, 64, 128], P(None, 'gx', 'gy')
- outlet_means: float32 [2, 64], replicated
Inputs may be any that keep to these rules, and one draw needn't show every extreme that they name: `populations`: positive. `cell_kind`: the plane z = 0 is all inlet (2), the plane z = 127 all outlet (3); all other cells are fluid (0) or wall (1). `outlet_region`: every region names at least one column; ids are constant on aligned tiles of 4 x 4 columns.
All inputs are finite; a program needn't handle non-finite values.
Results may differ from a plain program's by a relative error of at most 0.0001.
Values sent between devices are 32-bit elements; how exact they have to be, the bound alone decides.
A program may use at most 64 MiB of HBM per device.

v0:
```python
import jax
import jax.numpy as jnp
from jax import lax
from jax.sharding import PartitionSpec as P

REGIONS = 64
STEPS = 2
VELOCITIES = (
    (0, 0, 0),
    (1, 0, 0),
    (-1, 0, 0),
    (0, 1, 0),
    (0, -1, 0),
    (0, 0, 1),
    (0, 0, -1),
    (1, 1, 0),
    (-1, -1, 0),
    (1, -1, 0),
    (-1, 1, 0),
    (1, 0, 1),
    (-1, 0, -1),
    (1, 0, -1),
    (-1, 0, 1),
    (0, 1, 1),
    (0, -1, -1),
    (0, 1, -1),
    (0, -1, 1),
)
WEIGHTS = (1.0 / 3.0,) + (1.0 / 18.0,) * 6 + (1.0 / 36.0,) * 12
OPPOSITE = (0, 2, 1, 4, 3, 6, 5, 8, 7, 10, 9, 12, 11, 14, 13, 16, 15, 18, 17)
RELAX_TIME = 0.8
INLET_SPEED = 0.05
RISING_X = (1, 7, 9, 11, 13)
FALLING_X = (2, 8, 10, 12, 14)
RISING_Y = (3, 7, 10, 15, 17)
FALLING_Y = (4, 8, 9, 16, 18)


def from_behind(block, axis, distance):
    devices = range(lax.axis_size(axis))
    route = [(i - distance, i) for i in devices if i - distance in devices]
    return lax.ppermute(block, axis, route)


def from_behind_2(value, axis, steps):
    count = lax.axis_size(axis)
    pairs = [(source, (source + steps) % count) for source in range(count)]
    return lax.ppermute(value, axis, pairs)


def momentum(current, direction):
    total = jnp.zeros_like(current[0])
    for number in range(19):
        factor = VELOCITIES[number][direction]
        if factor != 0:
            total = total + factor * current[number]
    return total


def equilibrium(density, vel_x, vel_y, vel_z):
    speed_sq = vel_x * vel_x + vel_y * vel_y + vel_z * vel_z
    result = []
    for number in range(19):
        comp_x, comp_y, comp_z = VELOCITIES[number]
        projected = comp_x * vel_x + comp_y * vel_y + comp_z * vel_z
        result.append(
            WEIGHTS[number]
            * density
            * (1.0 + 3.0 * projected + 4.5 * projected * projected - 1.5 * speed_sq)
        )
    return jnp.stack(result)


def collide(current, kinds, col_mean):
    density = jnp.sum(current, axis=0)
    vel_x = momentum(current, 0) / density
    vel_y = momentum(current, 1) / density
    vel_z = momentum(current, 2) / density
    relaxed = current - (current - equilibrium(density, vel_x, vel_y, vel_z)) / RELAX_TIME
    bounced = jnp.stack([current[OPPOSITE[number]] for number in range(19)])
    unity = jnp.ones_like(density)
    still = jnp.zeros_like(density)
    inlet = equilibrium(unity, still, still, INLET_SPEED * unity)
    outlet = equilibrium(col_mean * unity, vel_x, vel_y, vel_z)
    post = jnp.where(kinds == 1, bounced, relaxed)
    post = jnp.where(kinds == 2, inlet, post)
    post = jnp.where(kinds == 3, outlet, post)
    return post


def stream(padded, rows_x, rows_y):
    moved = []
    for number in range(19):
        comp_x, comp_y, comp_z = VELOCITIES[number]
        plane = padded[
            number, 1 - comp_x : 1 - comp_x + rows_x, 1 - comp_y : 1 - comp_y + rows_y, :
        ]
        moved.append(jnp.roll(plane, comp_z, axis=2))
    return jnp.stack(moved)


def outlet_mean(current, kinds, onehot):
    density = jnp.sum(current, axis=0)
    is_outlet = kinds == 3
    column = jnp.sum(jnp.where(is_outlet, density, 0.0), axis=2).reshape(-1)
    col_count = jnp.sum(is_outlet.astype(jnp.float32), axis=2).reshape(-1)
    local_sums = jnp.dot(onehot, column, precision=lax.Precision.HIGHEST)
    local_counts = jnp.dot(onehot, col_count, precision=lax.Precision.HIGHEST)
    totals, counts = lax.psum((local_sums, local_counts), ("gx", "gy"))
    return totals / counts


def widen_first(post, from_lower, from_upper):
    blank = jnp.zeros_like(post[0, :1])
    planes = []
    for number in range(19):
        lower = from_lower[RISING_X.index(number)][None] if number in RISING_X else blank
        upper = from_upper[FALLING_X.index(number)][None] if number in FALLING_X else blank
        planes.append(jnp.concatenate([lower, post[number], upper], axis=0))
    return planes


def widen_second(planes, from_lower, from_upper):
    blank = jnp.zeros_like(planes[0][:, :1])
    padded = []
    for number in range(19):
        lower = from_lower[RISING_Y.index(number)][:, None] if number in RISING_Y else blank
        upper = from_upper[FALLING_Y.index(number)][:, None] if number in FALLING_Y else blank
        padded.append(jnp.concatenate([lower, planes[number], upper], axis=1))
    return jnp.stack(padded)


def body(populations, cell_kind, outlet_region):
    cells_x = populations.shape[1]
    cells_y = populations.shape[2]
    labels = jnp.arange(REGIONS, dtype=jnp.int32)
    onehot = (outlet_region.reshape(-1)[None, :] == labels[:, None]).astype(jnp.float32)
    current = populations
    means = []
    for timestep in range(STEPS):
        region_mean = outlet_mean(current, cell_kind, onehot)
        means.append(region_mean)
        col_mean = jnp.dot(region_mean, onehot, precision=lax.Precision.HIGHEST).reshape(
            cells_x, cells_y
        )[:, :, None]
        post = collide(current, cell_kind, col_mean)
        lower_x = from_behind(jnp.stack([post[number, -1] for number in RISING_X]), "gx", 1)
        upper_x = from_behind(jnp.stack([post[number, 0] for number in FALLING_X]), "gx", -1)
        planes = widen_first(post, lower_x, upper_x)
        lower_y = from_behind_2(jnp.stack([planes[number][:, -1] for number in RISING_Y]), "gy", 1)
        upper_y = from_behind_2(jnp.stack([planes[number][:, 0] for number in FALLING_Y]), "gy", -1)
        padded = widen_second(planes, lower_y, upper_y)
        current = stream(padded, cells_x, cells_y)
    return (current, jnp.stack(means))


def solution(mesh):
    in_specs = (P(None, "gx", "gy", None), P("gx", "gy", None), P("gx", "gy"))
    out_specs = (P(None, "gx", "gy", None), P())
    return jax.shard_map(body, mesh=mesh, in_specs=in_specs, out_specs=out_specs, check_vma=False)
```

profile of v0, /device:TPU:1, one launch (start us, length us, event | category | flops | bytes accessed | tf_op | source)
XLA Modules:
  0.0 127.7 jit_solution(15017054482665278097)
XLA Ops:
  0.7 0.8 constant_dynamic-update-slice_fusion.47
  1.5 1.1 reduce_sum.854
  2.7 0.7 copy-done.1
  4.1 0.6 copy-done.2
  4.9 0.2 convolution_bitcast_fusion.4
  5.1 40.5 %all-reduce = (f32[64]{0:T(128)S(1)}, f32[64]{0:T(128)S(1)}) all-reduce(f32[64]{0:T(128)S(1)} %convolution_bitcast_fusion.4, f32[64]{0:T(128)S(1)} %convolution_bitcast_fusion.3), channel_id=1, replica_groups=mesh['gx'=4,'gy'=8] {'gx','gy'}, use_global_device_ids=true, to_apply=%region_2.3 | all-reduce | flops 128 | bytes 1024 | tf_op jit(solution)/shard_map/psum | solution.py:109
  47.8 0.3 select_select_fusion.1
  48.2 5.3 %collective-permute-start = (f32[5,8,128]{2,1,0:T(8,128)S(1)}, f32[5,8,128]{2,1,0:T(8,128)S(1)}, u32[]{:S(2)}, u32[]{:S(2)}) collective-permute-start(f32[5,8,128]{2,1,0:T(8,128)S(1)} %get-tuple-element.153), channel_id=1, source_target_pairs={{0,8},{8,16},{16,24},{1,9},{9,17},{17,25},{2,10},{10,18},{18,26},{... | collective-permute-start | bytes 61448 | tf_op jit(solution)/shard_map/ppermute | solution.py:42
  53.5 1.9 %collective-permute-start.1 = (f32[5,8,128]{2,1,0:T(8,128)S(1)}, f32[5,8,128]{2,1,0:T(8,128)S(1)}, u32[]{:S(2)}, u32[]{:S(2)}) collective-permute-start(f32[5,8,128]{2,1,0:T(8,128)S(1)} %get-tuple-element.154), channel_id=1, source_target_pairs={{8,0},{16,8},{24,16},{9,1},{17,9},{25,17},{10,2},{18,10},{26,18},{... | collective-permute-start | bytes 61448 | tf_op jit(solution)/shard_map/ppermute | solution.py:42
  55.5 3.1 %collective-permute-done.1 = f32[5,8,128]{2,1,0:T(8,128)S(1)} collective-permute-done((f32[5,8,128]{2,1,0:T(8,128)S(1)}, f32[5,8,128]{2,1,0:T(8,128)S(1)}, u32[]{:S(2)}, u32[]{:S(2)}) %collective-permute-start.1) | collective-permute-done | bytes 20512 | tf_op jit(solution)/shard_map/ppermute | solution.py:42
  58.7 0.3 collective-permute-start.2
  59.2 4.0 %collective-permute-start.3 = (f32[5,10,128]{2,0,1:T(8,128)S(1)}, f32[5,10,128]{2,0,1:T(8,128)S(1)}, u32[]{:S(2)}, u32[]{:S(2)}) collective-permute-start(f32[5,10,128]{2,0,1:T(8,128)S(1)} %stack.147), channel_id=1, source_target_pairs={{0,7},{1,0},{2,1},{3,2},{4,3},{5,4},{6,5},{7,6},{8,15},{9,8},{10,9... | collective-permute-start | bytes 76808 | tf_op jit(solution)/shard_map/ppermute | solution.py:48
  63.2 1.1 collective-permute-done.2
  65.7 0.3 constant_dynamic-update-slice_fusion.152
  67.2 38.7 %psum.26 = f32[64]{0:T(128)S(1)} all-reduce(f32[64]{0:T(128)S(1)} %convolution_bitcast_fusion.1), channel_id=1, replica_groups=mesh['gx'=4,'gy'=8] {'gx','gy'}, use_global_device_ids=true, to_apply=%region_6.7 | all-reduce | flops 64 | bytes 512 | tf_op jit(solution)/shard_map/psum | solution.py:109
  107.7 0.3 select_select_fusion
  108.2 5.3 %collective-permute-start.4 = (f32[5,8,128]{2,1,0:T(8,128)S(1)}, f32[5,8,128]{2,1,0:T(8,128)S(1)}, u32[]{:S(2)}, u32[]{:S(2)}) collective-permute-start(f32[5,8,128]{2,1,0:T(8,128)S(1)} %get-tuple-element.125), channel_id=1, source_target_pairs={{0,8},{8,16},{16,24},{1,9},{9,17},{17,25},{2,10},{10,18},{18,26},{... | collective-permute-start | bytes 61448 | tf_op jit(solution)/shard_map/ppermute | solution.py:42
  113.4 1.9 %collective-permute-start.5 = (f32[5,8,128]{2,1,0:T(8,128)S(1)}, f32[5,8,128]{2,1,0:T(8,128)S(1)}, u32[]{:S(2)}, u32[]{:S(2)}) collective-permute-start(f32[5,8,128]{2,1,0:T(8,128)S(1)} %get-tuple-element.124), channel_id=1, source_target_pairs={{8,0},{16,8},{24,16},{9,1},{17,9},{25,17},{10,2},{18,10},{26,18},{... | collective-permute-start | bytes 61448 | tf_op jit(solution)/shard_map/ppermute | solution.py:42
  115.4 0.6 pad_maximum_fusion.164
  116.0 2.6 %collective-permute-done.5 = f32[5,8,128]{2,1,0:T(8,128)S(1)} collective-permute-done((f32[5,8,128]{2,1,0:T(8,128)S(1)}, f32[5,8,128]{2,1,0:T(8,128)S(1)}, u32[]{:S(2)}, u32[]{:S(2)}) %collective-permute-start.5) | collective-permute-done | bytes 20512 | tf_op jit(solution)/shard_map/ppermute | solution.py:42
  118.7 0.8 collective-permute-start.7
  119.5 0.7 collective-permute-start.6
  120.7 4.5 %collective-permute-done.6 = f32[5,10,128]{2,0,1:T(8,128)S(1)} collective-permute-done((f32[5,10,128]{2,0,1:T(8,128)S(1)}, f32[5,10,128]{2,0,1:T(8,128)S(1)}, u32[]{:S(2)}, u32[]{:S(2)}) %collective-permute-start.6) | collective-permute-done | bytes 25632 | tf_op jit(solution)/shard_map/ppermute | solution.py:48
  126.9 0.8 copy-done.3
  (271 shorter events, 9.3 us)
Async XLA Ops:
  0.6 2.0 %copy-start = (f32[19,8,8,128]{3,2,1,0:T(8,128)S(1)}, f32[19,8,8,128]{3,2,1,0:T(8,128)}, u32[]{:S(2)}) copy-start(f32[19,8,8,128]{3,2,1,0:T(8,128)} %param.3) | copy-start | bytes 1867780
  2.6 0.8 copy-start.1
  4.0 0.7 copy-start.2
  48.2 10.4 %collective-permute-start = (f32[5,8,128]{2,1,0:T(8,128)S(1)}, f32[5,8,128]{2,1,0:T(8,128)S(1)}, u32[]{:S(2)}, u32[]{:S(2)}) collective-permute-start(f32[5,8,128]{2,1,0:T(8,128)S(1)} %get-tuple-element.153), channel_id=1, source_target_pairs={{0,8},{8,16},{16,24},{1,9},{9,17},{17,25},{2,10},{10,18},{18,26},{... | collective-permute-start | bytes 61448 | tf_op jit(solution)/shard_map/ppermute | solution.py:42
  53.5 5.1 %collective-permute-start.1 = (f32[5,8,128]{2,1,0:T(8,128)S(1)}, f32[5,8,128]{2,1,0:T(8,128)S(1)}, u32[]{:S(2)}, u32[]{:S(2)}) collective-permute-start(f32[5,8,128]{2,1,0:T(8,128)S(1)} %get-tuple-element.154), channel_id=1, source_target_pairs={{8,0},{16,8},{24,16},{9,1},{17,9},{25,17},{10,2},{18,10},{26,18},{... | collective-permute-start | bytes 61448 | tf_op jit(solution)/shard_map/ppermute | solution.py:42
  58.7 5.6 %collective-permute-start.2 = (f32[5,10,128]{2,0,1:T(8,128)S(1)}, f32[5,10,128]{2,0,1:T(8,128)S(1)}, u32[]{:S(2)}, u32[]{:S(2)}) collective-permute-start(f32[5,10,128]{2,0,1:T(8,128)S(1)} %stack.145), channel_id=1, source_target_pairs={{0,1},{1,2},{2,3},{3,4},{4,5},{5,6},{6,7},{7,0},{8,9},{9,10},{10,1... | collective-permute-start | bytes 76808 | tf_op jit(solution)/shard_map/ppermute | solution.py:48
  59.2 5.2 %collective-permute-start.3 = (f32[5,10,128]{2,0,1:T(8,128)S(1)}, f32[5,10,128]{2,0,1:T(8,128)S(1)}, u32[]{:S(2)}, u32[]{:S(2)}) collective-permute-start(f32[5,10,128]{2,0,1:T(8,128)S(1)} %stack.147), channel_id=1, source_target_pairs={{0,7},{1,0},{2,1},{3,2},{4,3},{5,4},{6,5},{7,6},{8,15},{9,8},{10,9... | collective-permute-start | bytes 76808 | tf_op jit(solution)/shard_map/ppermute | solution.py:48
  108.2 7.8 %collective-permute-start.4 = (f32[5,8,128]{2,1,0:T(8,128)S(1)}, f32[5,8,128]{2,1,0:T(8,128)S(1)}, u32[]{:S(2)}, u32[]{:S(2)}) collective-permute-start(f32[5,8,128]{2,1,0:T(8,128)S(1)} %get-tuple-element.125), channel_id=1, source_target_pairs={{0,8},{8,16},{16,24},{1,9},{9,17},{17,25},{2,10},{10,18},{18,26},{... | collective-permute-start | bytes 61448 | tf_op jit(solution)/shard_map/ppermute | solution.py:42
  113.4 5.1 %collective-permute-start.5 = (f32[5,8,128]{2,1,0:T(8,128)S(1)}, f32[5,8,128]{2,1,0:T(8,128)S(1)}, u32[]{:S(2)}, u32[]{:S(2)}) collective-permute-start(f32[5,8,128]{2,1,0:T(8,128)S(1)} %get-tuple-element.124), channel_id=1, source_target_pairs={{8,0},{16,8},{24,16},{9,1},{17,9},{25,17},{10,2},{18,10},{26,18},{... | collective-permute-start | bytes 61448 | tf_op jit(solution)/shard_map/ppermute | solution.py:42
  118.7 6.9 %collective-permute-start.7 = (f32[5,10,128]{2,0,1:T(8,128)S(1)}, f32[5,10,128]{2,0,1:T(8,128)S(1)}, u32[]{:S(2)}, u32[]{:S(2)}) collective-permute-start(f32[5,10,128]{2,0,1:T(8,128)S(1)} %stack.347), channel_id=1, source_target_pairs={{0,7},{1,0},{2,1},{3,2},{4,3},{5,4},{6,5},{7,6},{8,15},{9,8},{10,9... | collective-permute-start | bytes 76808 | tf_op jit(solution)/shard_map/ppermute | solution.py:48
  119.5 5.6 %collective-permute-start.6 = (f32[5,10,128]{2,0,1:T(8,128)S(1)}, f32[5,10,128]{2,0,1:T(8,128)S(1)}, u32[]{:S(2)}, u32[]{:S(2)}) collective-permute-start(f32[5,10,128]{2,0,1:T(8,128)S(1)} %stack.172), channel_id=1, source_target_pairs={{0,1},{1,2},{2,3},{3,4},{4,5},{5,6},{6,7},{7,0},{8,9},{9,10},{10,1... | collective-permute-start | bytes 76808 | tf_op jit(solution)/shard_map/ppermute | solution.py:48
  126.9 0.8 copy-start.3
where the time goes:
time: 128 us
  blocking collectives  79.2 us (62%)
  starting transfers between devices  20.2 us (16%)
  waiting for transfers between devices  11.3 us (9%)
  other arithmetic  8.05 us (6%)
  local copies, waits for them, and re-layouts  6.31 us (5%)
  between operations  2.01 us (2%)
    psum x2, blocking collectives, outlet_mean(): totals, counts = lax.psum((local_sums, local_counts), ('gx', 'gy'))  79.2 us
    ppermute x4, starting transfers between devices, from_behind(): return lax.ppermute(block, axis, route)  14.4 us
    ppermute x4, starting transfers between devices, from_behind_2(): return lax.ppermute(value, axis, pairs)  5.84 us
    ppermute x4, waiting for transfers between devices, from_behind(): return lax.ppermute(block, axis, route)  5.67 us
    ppermute x4, waiting for transfers between devices, from_behind_2(): return lax.ppermute(value, axis, pairs)  5.62 us
    unnamed x80, other arithmetic  4.53 us
    unnamed x79, local copies, waits for them, and re-layouts  3.4 us
  transfers between devices with their start and end apart: 8, of which 4 were waited for; matrix products, arithmetic and copies ran while one was open for 1% of the time, Pallas kernels for 0%

commit v1 on v0

--- a/solution.py
+++ b/solution.py
@@ -106,7 +106,7 @@
     col_count = jnp.sum(is_outlet.astype(jnp.float32), axis=2).reshape(-1)
     local_sums = jnp.dot(onehot, column, precision=lax.Precision.HIGHEST)
     local_counts = jnp.dot(onehot, col_count, precision=lax.Precision.HIGHEST)
-    totals, counts = lax.psum((local_sums, local_counts), ("gx", "gy"))
+    totals, counts = lax.psum(lax.psum((local_sums, local_counts), "gy"), "gx")
     return totals / counts
 
 

time: 128 us -> 100 us (0.78)
  blocking collectives: 79.2 us -> 55.1 us
  starting transfers between devices: 20.2 us -> 17.4 us
    psum x2 -> x4, blocking collectives: 79.2 us -> 55.1 us  [outlet_mean(): totals, counts = lax.psum(lax.psum((local_sums, local_counts), 'gy'), 'gx')]
    ppermute x4, starting transfers between devices: 14.4 us -> 11.6 us  [from_behind(): return lax.ppermute(block, axis, route)]
  transfers between devices with their start and end apart: 8 -> 8, of which waited for: 4 -> 4; matrix products, arithmetic and copies ran while one was open for 1% -> 2% of each run, Pallas kernels for 0% -> 0%
where the time goes in v1:
time: 100 us
  blocking collectives  55.1 us (55%)
  starting transfers between devices  17.4 us (17%)
  waiting for transfers between devices  10.5 us (10%)
  other arithmetic  8.06 us (8%)
  local copies, waits for them, and re-layouts  6.31 us (6%)
  between operations  2.03 us (2%)
    psum x4, blocking collectives, outlet_mean(): totals, counts = lax.psum(lax.psum((local_sums, local_counts), 'gy'), 'gx')  55.1 us
    ppermute x4, starting transfers between devices, from_behind(): return lax.ppermute(block, axis, route)  11.6 us
    ppermute x4, starting transfers between devices, from_behind_2(): return lax.ppermute(value, axis, pairs)  5.81 us
    ppermute x4, waiting for transfers between devices, from_behind(): return lax.ppermute(block, axis, route)  5.67 us
    ppermute x4, waiting for transfers between devices, from_behind_2(): return lax.ppermute(value, axis, pairs)  4.86 us
    unnamed x80, other arithmetic  4.53 us
    unnamed x79, local copies, waits for them, and re-layouts  3.41 us
  transfers between devices with their start and end apart: 8, of which 4 were waited for; matrix products, arithmetic and copies ran while one was open for 2% of the time, Pallas kernels for 0%

profile of v1, /device:TPU:1, one launch (start us, length us, event | category | flops | bytes accessed | tf_op | source)
XLA Modules:
  0.0 100.1 jit_solution(11535391032427421951)
XLA Ops:
  0.7 0.8 constant_dynamic-update-slice_fusion.47
  1.5 1.1 %reduce_sum.854 = f32[8,8,128]{2,1,0:T(8,128)S(1)} reduce(f32[19,8,8,128]{3,2,1,0:T(8,128)} %param.3, f32[]{:T(128)} %constant.20.clone.1), dimensions={0}, to_apply=%region_0.0 | reduce | flops 147456 | bytes 655364 | tf_op jit(solution)/shard_map/reduce_sum | solution.py:103
  2.7 0.7 copy-done.1
  4.1 0.6 copy-done.2
  4.9 0.2 convolution_bitcast_fusion.4
  5.1 18.8 %all-reduce = (f32[64]{0:T(128)S(1)}, f32[64]{0:T(128)S(1)}) all-reduce(f32[64]{0:T(128)S(1)} %convolution_bitcast_fusion.4, f32[64]{0:T(128)S(1)} %convolution_bitcast_fusion.3), channel_id=1, replica_groups=mesh['gx'=4,'gy'=8] {'gy'}, use_global_device_ids=true, to_apply=%region_2.3 | all-reduce | flops 128 | bytes 1024 | tf_op jit(solution)/shard_map/psum | solution.py:109
  23.9 9.4 %all-reduce.1 = (f32[64]{0:T(128)S(1)}, f32[64]{0:T(128)S(1)}) all-reduce(f32[64]{0:T(128)S(1)} %get-tuple-element.6, f32[64]{0:T(128)S(1)} %get-tuple-element.7), channel_id=1, replica_groups=mesh['gx'=4,'gy'=8] {'gx'}, use_global_device_ids=true, to_apply=%region_3.4 | all-reduce | flops 128 | bytes 1024 | tf_op jit(solution)/shard_map/psum | solution.py:109
  35.5 0.3 select_select_fusion.1
  35.9 3.9 %collective-permute-start = (f32[5,8,128]{2,1,0:T(8,128)S(1)}, f32[5,8,128]{2,1,0:T(8,128)S(1)}, u32[]{:S(2)}, u32[]{:S(2)}) collective-permute-start(f32[5,8,128]{2,1,0:T(8,128)S(1)} %get-tuple-element.155), channel_id=1, source_target_pairs={{0,8},{8,16},{16,24},{1,9},{9,17},{17,25},{2,10},{10,18},{18,26},{... | collective-permute-start | bytes 61448 | tf_op jit(solution)/shard_map/ppermute | solution.py:42
  39.8 1.9 %collective-permute-start.1 = (f32[5,8,128]{2,1,0:T(8,128)S(1)}, f32[5,8,128]{2,1,0:T(8,128)S(1)}, u32[]{:S(2)}, u32[]{:S(2)}) collective-permute-start(f32[5,8,128]{2,1,0:T(8,128)S(1)} %get-tuple-element.156), channel_id=1, source_target_pairs={{8,0},{16,8},{24,16},{9,1},{17,9},{25,17},{10,2},{18,10},{26,18},{... | collective-permute-start | bytes 61448 | tf_op jit(solution)/shard_map/ppermute | solution.py:42
  41.8 3.1 %collective-permute-done.1 = f32[5,8,128]{2,1,0:T(8,128)S(1)} collective-permute-done((f32[5,8,128]{2,1,0:T(8,128)S(1)}, f32[5,8,128]{2,1,0:T(8,128)S(1)}, u32[]{:S(2)}, u32[]{:S(2)}) %collective-permute-start.1) | collective-permute-done | bytes 20512 | tf_op jit(solution)/shard_map/ppermute | solution.py:42
  45.3 4.2 %collective-permute-start.3 = (f32[5,10,128]{2,0,1:T(8,128)S(1)}, f32[5,10,128]{2,0,1:T(8,128)S(1)}, u32[]{:S(2)}, u32[]{:S(2)}) collective-permute-start(f32[5,10,128]{2,0,1:T(8,128)S(1)} %stack.147), channel_id=1, source_target_pairs={{0,7},{1,0},{2,1},{3,2},{4,3},{5,4},{6,5},{7,6},{8,15},{9,8},{10,9... | collective-permute-start | bytes 76808 | tf_op jit(solution)/shard_map/ppermute | solution.py:48
  49.5 1.1 %collective-permute-done.2 = f32[5,10,128]{2,0,1:T(8,128)S(1)} collective-permute-done((f32[5,10,128]{2,0,1:T(8,128)S(1)}, f32[5,10,128]{2,0,1:T(8,128)S(1)}, u32[]{:S(2)}, u32[]{:S(2)}) %collective-permute-start.2) | collective-permute-done | bytes 25632 | tf_op jit(solution)/shard_map/ppermute | solution.py:48
  52.0 0.3 constant_dynamic-update-slice_fusion.152
  53.5 18.1 %psum.52 = f32[64]{0:T(128)S(1)} all-reduce(f32[64]{0:T(128)S(1)} %convolution_bitcast_fusion.1), channel_id=1, replica_groups=mesh['gx'=4,'gy'=8] {'gy'}, use_global_device_ids=true, to_apply=%region_8.9 | all-reduce | flops 64 | bytes 512 | tf_op jit(solution)/shard_map/psum | solution.py:109
  71.6 8.8 %psum.53 = f32[64]{0:T(128)S(1)} all-reduce(f32[64]{0:T(128)S(1)} %psum.52), channel_id=1, replica_groups=mesh['gx'=4,'gy'=8] {'gx'}, use_global_device_ids=true, to_apply=%region_9.10 | all-reduce | flops 64 | bytes 512 | tf_op jit(solution)/shard_map/psum | solution.py:109
  82.2 0.3 select_select_fusion
  82.7 3.9 %collective-permute-start.4 = (f32[5,8,128]{2,1,0:T(8,128)S(1)}, f32[5,8,128]{2,1,0:T(8,128)S(1)}, u32[]{:S(2)}, u32[]{:S(2)}) collective-permute-start(f32[5,8,128]{2,1,0:T(8,128)S(1)} %get-tuple-element.127), channel_id=1, source_target_pairs={{0,8},{8,16},{16,24},{1,9},{9,17},{17,25},{2,10},{10,18},{18,26},{... | collective-permute-start | bytes 61448 | tf_op jit(solution)/shard_map/ppermute | solution.py:42
  86.6 1.9 %collective-permute-start.5 = (f32[5,8,128]{2,1,0:T(8,128)S(1)}, f32[5,8,128]{2,1,0:T(8,128)S(1)}, u32[]{:S(2)}, u32[]{:S(2)}) collective-permute-start(f32[5,8,128]{2,1,0:T(8,128)S(1)} %get-tuple-element.126), channel_id=1, source_target_pairs={{8,0},{16,8},{24,16},{9,1},{17,9},{25,17},{10,2},{18,10},{26,18},{... | collective-permute-start | bytes 61448 | tf_op jit(solution)/shard_map/ppermute | solution.py:42
  88.5 0.6 pad_maximum_fusion.164
  89.1 2.6 %collective-permute-done.5 = f32[5,8,128]{2,1,0:T(8,128)S(1)} collective-permute-done((f32[5,8,128]{2,1,0:T(8,128)S(1)}, f32[5,8,128]{2,1,0:T(8,128)S(1)}, u32[]{:S(2)}, u32[]{:S(2)}) %collective-permute-start.5) | collective-permute-done | bytes 20512 | tf_op jit(solution)/shard_map/ppermute | solution.py:42
  91.9 1.5 %collective-permute-start.6 = (f32[5,10,128]{2,0,1:T(8,128)S(1)}, f32[5,10,128]{2,0,1:T(8,128)S(1)}, u32[]{:S(2)}, u32[]{:S(2)}) collective-permute-start(f32[5,10,128]{2,0,1:T(8,128)S(1)} %stack.172), channel_id=1, source_target_pairs={{0,1},{1,2},{2,3},{3,4},{4,5},{5,6},{6,7},{7,0},{8,9},{9,10},{10,1... | collective-permute-start | bytes 76808 | tf_op jit(solution)/shard_map/ppermute | solution.py:48
  93.8 3.7 %collective-permute-done.6 = f32[5,10,128]{2,0,1:T(8,128)S(1)} collective-permute-done((f32[5,10,128]{2,0,1:T(8,128)S(1)}, f32[5,10,128]{2,0,1:T(8,128)S(1)}, u32[]{:S(2)}, u32[]{:S(2)}) %collective-permute-start.6) | collective-permute-done | bytes 25632 | tf_op jit(solution)/shard_map/ppermute | solution.py:48
  99.3 0.8 copy-done.3
  (273 shorter events, 9.4 us)
Async XLA Ops:
  0.6 2.0 %copy-start = (f32[19,8,8,128]{3,2,1,0:T(8,128)S(1)}, f32[19,8,8,128]{3,2,1,0:T(8,128)}, u32[]{:S(2)}) copy-start(f32[19,8,8,128]{3,2,1,0:T(8,128)} %param.3) | copy-start | bytes 1867780
  2.6 0.8 copy-start.1
  4.0 0.7 copy-start.2
  35.9 9.0 %collective-permute-start = (f32[5,8,128]{2,1,0:T(8,128)S(1)}, f32[5,8,128]{2,1,0:T(8,128)S(1)}, u32[]{:S(2)}, u32[]{:S(2)}) collective-permute-start(f32[5,8,128]{2,1,0:T(8,128)S(1)} %get-tuple-element.155), channel_id=1, source_target_pairs={{0,8},{8,16},{16,24},{1,9},{9,17},{17,25},{2,10},{10,18},{18,26},{... | collective-permute-start | bytes 61448 | tf_op jit(solution)/shard_map/ppermute | solution.py:42
  39.8 5.1 %collective-permute-start.1 = (f32[5,8,128]{2,1,0:T(8,128)S(1)}, f32[5,8,128]{2,1,0:T(8,128)S(1)}, u32[]{:S(2)}, u32[]{:S(2)}) collective-permute-start(f32[5,8,128]{2,1,0:T(8,128)S(1)} %get-tuple-element.156), channel_id=1, source_target_pairs={{8,0},{16,8},{24,16},{9,1},{17,9},{25,17},{10,2},{18,10},{26,18},{... | collective-permute-start | bytes 61448 | tf_op jit(solution)/shard_map/ppermute | solution.py:42
  45.0 5.6 %collective-permute-start.2 = (f32[5,10,128]{2,0,1:T(8,128)S(1)}, f32[5,10,128]{2,0,1:T(8,128)S(1)}, u32[]{:S(2)}, u32[]{:S(2)}) collective-permute-start(f32[5,10,128]{2,0,1:T(8,128)S(1)} %stack.145), channel_id=1, source_target_pairs={{0,1},{1,2},{2,3},{3,4},{4,5},{5,6},{6,7},{7,0},{8,9},{9,10},{10,1... | collective-permute-start | bytes 76808 | tf_op jit(solution)/shard_map/ppermute | solution.py:48
  45.3 5.5 %collective-permute-start.3 = (f32[5,10,128]{2,0,1:T(8,128)S(1)}, f32[5,10,128]{2,0,1:T(8,128)S(1)}, u32[]{:S(2)}, u32[]{:S(2)}) collective-permute-start(f32[5,10,128]{2,0,1:T(8,128)S(1)} %stack.147), channel_id=1, source_target_pairs={{0,7},{1,0},{2,1},{3,2},{4,3},{5,4},{6,5},{7,6},{8,15},{9,8},{10,9... | collective-permute-start | bytes 76808 | tf_op jit(solution)/shard_map/ppermute | solution.py:48
  82.7 6.4 %collective-permute-start.4 = (f32[5,8,128]{2,1,0:T(8,128)S(1)}, f32[5,8,128]{2,1,0:T(8,128)S(1)}, u32[]{:S(2)}, u32[]{:S(2)}) collective-permute-start(f32[5,8,128]{2,1,0:T(8,128)S(1)} %get-tuple-element.127), channel_id=1, source_target_pairs={{0,8},{8,16},{16,24},{1,9},{9,17},{17,25},{2,10},{10,18},{18,26},{... | collective-permute-start | bytes 61448 | tf_op jit(solution)/shard_map/ppermute | solution.py:42
  86.6 5.1 %collective-permute-start.5 = (f32[5,8,128]{2,1,0:T(8,128)S(1)}, f32[5,8,128]{2,1,0:T(8,128)S(1)}, u32[]{:S(2)}, u32[]{:S(2)}) collective-permute-start(f32[5,8,128]{2,1,0:T(8,128)S(1)} %get-tuple-element.126), channel_id=1, source_target_pairs={{8,0},{16,8},{24,16},{9,1},{17,9},{25,17},{10,2},{18,10},{26,18},{... | collective-permute-start | bytes 61448 | tf_op jit(solution)/shard_map/ppermute | solution.py:42
  91.8 6.2 %collective-permute-start.7 = (f32[5,10,128]{2,0,1:T(8,128)S(1)}, f32[5,10,128]{2,0,1:T(8,128)S(1)}, u32[]{:S(2)}, u32[]{:S(2)}) collective-permute-start(f32[5,10,128]{2,0,1:T(8,128)S(1)} %stack.347), channel_id=1, source_target_pairs={{0,7},{1,0},{2,1},{3,2},{4,3},{5,4},{6,5},{7,6},{8,15},{9,8},{10,9... | collective-permute-start | bytes 76808 | tf_op jit(solution)/shard_map/ppermute | solution.py:48
  91.9 5.6 %collective-permute-start.6 = (f32[5,10,128]{2,0,1:T(8,128)S(1)}, f32[5,10,128]{2,0,1:T(8,128)S(1)}, u32[]{:S(2)}, u32[]{:S(2)}) collective-permute-start(f32[5,10,128]{2,0,1:T(8,128)S(1)} %stack.172), channel_id=1, source_target_pairs={{0,1},{1,2},{2,3},{3,4},{4,5},{5,6},{6,7},{7,0},{8,9},{9,10},{10,1... | collective-permute-start | bytes 76808 | tf_op jit(solution)/shard_map/ppermute | solution.py:48
  99.3 0.8 copy-start.3
